TPU v7x, 32 devices: a whole 2x2x4 slice. The times are simulated.
32 devices in a mesh: seq: 8 (over z, y), head: 4 (over x, core).
Axes of the slice: x: 2, y: 2, z: 4, core: 2. Of those that a mesh axis runs over, the one named last changes fastest.
Arguments:
- hidden_states: bfloat16 [8, 512, 3584], P(None, 'seq', 'head'), may hold values from -6 to 6
- boundary: int32 [8, 64], replicated, may hold values from 0 to 511, as said below
- valid: int32 [8, 64], replicated, may hold values from 0 to 1, as said below
- pairs: int32 [8, 2], replicated, may hold values from 0 to 7, as said below
- w_first: bfloat16 [3584, 4096], P('seq', 'head'), may hold values from -0.09375 to 0.09375
- b_first: float32 [4096], P('head'), may hold values from -3 to 3
- w_second: float32 [4096], P('head'), may hold values from -0.09375 to 0.09375
Outputs:
- step_reward: float32 [8, 64], replicated
- trace_score: float32 [8], replicated
- margin: float32 [8], replicated
Inputs may be any that keep to these rules, and one draw needn't show every extreme that they name: Within a trace the 64 boundary positions are distinct and increasing. In each trace the ones come first; every trace has 16 to 64 valid steps. `pairs`: the two traces of a pair differ.
All inputs are finite; a program needn't handle non-finite values.
Results may differ from a plain program's by a relative error of at most 0.0003.
Values may be sent and summed in bfloat16 or wider, within the bound.
A program may use at most 64 MiB of HBM per device.

v0:
```python
import jax
import jax.numpy as jnp
from jax import lax
from jax.sharding import PartitionSpec as P


def score_rows(rows, w_first, b_first, w_second):
    pre = jnp.dot(
        rows, lax.all_gather(w_first, "seq", axis=0, tiled=True), preferred_element_type=jnp.float32
    )
    return jnp.sum(jnp.maximum(pre + b_first, 0.0) * w_second, axis=-1)


def per_device(hidden_states, boundary, valid, pairs, w_first, b_first, w_second):
    traces, tok_dev, quarter = hidden_states.shape
    offset = lax.axis_index("seq") * tok_dev
    positions = offset + jnp.arange(tok_dev, dtype=jnp.int32)
    hits = boundary[:, :, None] == positions[None, None, :]
    whole = lax.all_gather(hidden_states, "head", axis=2, tiled=True)
    token_logit = score_rows(
        whole.reshape(traces * tok_dev, whole.shape[2]), w_first, b_first, w_second
    )
    token_logit = token_logit.reshape(traces, tok_dev)
    partial_logit = jnp.sum(jnp.where(hits, token_logit[:, None, :], 0.0), axis=2)
    logit = lax.psum(partial_logit, ("seq", "head"))
    live = valid == 1
    step_reward = jnp.where(live, logit, jnp.float32(0.0))
    trace_score = jnp.min(jnp.where(live, logit, jnp.float32(1e30)), axis=1)
    trace_ids = jnp.arange(traces, dtype=jnp.int32)[None, :]
    winner = jnp.sum(jnp.where(pairs[:, 0:1] == trace_ids, trace_score[None, :], 0.0), axis=1)
    loser = jnp.sum(jnp.where(pairs[:, 1:2] == trace_ids, trace_score[None, :], 0.0), axis=1)
    return (step_reward, trace_score, winner - loser)


def solution(mesh):
    placed = (P(None, "seq", "head"), P(), P(), P(), P("seq", "head"), P("head"), P("head"))
    return jax.shard_map(
        per_device, mesh=mesh, in_specs=placed, out_specs=(P(), P(), P()), check_vma=False
    )
```

profile of v0, /device:TPU:0, one launch (start us, length us, event | category | flops | bytes accessed | tf_op | source)
XLA Modules:
  0.0 212.7 jit_solution(10916989333486681788)
XLA Ops:
  7.2 0.0 all-gather.3.cloned.1.call-start
  7.2 0.7 all-gather.3.cloned.1.call-update
  7.9 0.0 all-gather.5.cloned.1.call-start
  7.9 0.7 all-gather.5.cloned.1.call-update
  8.7 0.8 slice_bitcast_fusion.1
  9.4 34.3 %all-gather.3.cloned.1.call-done = bf16[8,64,3584]{2,1,0:T(8,128)(2,1)} async-done(((bf16[8,64,896]{2,1,0:T(8,128)(2,1)}), bf16[8,64,3584]{2,1,0:T(8,128)(2,1)}) %all-gather.3.cloned.1.call-update) | async-done | bytes 3670032 | tf_op jit(solution)/shard_map/all_gather | solution.py:19
  43.8 113.7 %all-gather.5.cloned.1.call-done = bf16[3584,1024]{1,0:T(8,128)(2,1)} async-done(((bf16[448,1024]{1,0:T(8,128)(2,1)}), bf16[3584,1024]{1,0:T(8,128)(2,1)}) %all-gather.5.cloned.1.call-update) | async-done | bytes 7340048 | tf_op jit(solution)/shard_map/all_gather | solution.py:9
  157.5 0.0 copy-start
  157.5 0.0 copy-start.1
  157.5 8.2 %multiply_reduce_fusion = f32[512]{0:T(512)S(1)} fusion(bf16[512,3584]{1,0:T(8,128)(2,1)} %bitcast.7, bf16[3584,1024]{1,0:T(8,128)(2,1)} %all-gather.5.cloned.1.call-done, f32[1024]{0:T(1024)} %param.13, f32[1024]{0:T(1024)} %param.12), kind=kOutput, calls=%fused_computation | convolution fusion | flops 3760193024 | bytes 11020288 | tf_op jit(solution)/shard_map/dot_general | solution.py:8
  165.7 0.1 broadcast_in_dim.44
  165.7 0.0 copy-done
  165.7 0.3 select_reduce_fusion
  166.0 38.4 %psum.7 = f32[8,64]{1,0:T(8,128)S(1)} all-reduce(f32[8,64]{1,0:T(8,128)S(1)} %select_reduce_fusion), channel_id=1, replica_groups=mesh['seq'=8,'head'=4] {'seq','head'}, use_global_device_ids=true, to_apply=%region_2.3 | all-reduce | flops 512 | bytes 4096 | tf_op jit(solution)/shard_map/psum | solution.py:25
  204.4 0.0 copy-done.1
  204.4 0.1 select_reduce_fusion.3
  204.5 0.0 copy-start.2
  204.5 0.6 broadcast_select_fusion
  205.1 0.2 select_reduce_fusion.1
  205.4 0.5 sub.3
  205.9 0.0 copy-done.2
  (1 shorter events, 0.0 us)
Async XLA Ops:
  7.2 36.6 %all-gather.3.cloned.1.call-start = ((), (), s32[]{:S(2)}) async-start(), calls=%async_computation | async-start | bytes 4587520 | tf_op jit(solution)/shard_map/all_gather | solution.py:19
  7.9 149.6 %all-gather.5.cloned.1.call-start = ((), (), s32[]{:S(2)}) async-start(), calls=%async_computation.1 | async-start | bytes 8257536 | tf_op jit(solution)/shard_map/all_gather | solution.py:9
  157.5 8.3 %copy-start = (s32[8,64]{1,0:T(8,128)S(1)}, s32[8,64]{1,0:T(8,128)}, u32[]{:S(2)}) copy-start(s32[8,64]{1,0:T(8,128)} %param.8) | copy-start | bytes 6148
  157.5 47.0 %copy-start.1 = (s32[8,64]{1,0:T(8,128)S(1)}, s32[8,64]{1,0:T(8,128)}, u32[]{:S(2)}) copy-start(s32[8,64]{1,0:T(8,128)} %param.9) | copy-start | bytes 6148
  204.5 1.3 copy-start.2
Sparse Core Ops, SparseCore 0:
  9.5 34.1 all-gather.2
  45.9 111.4 all-gather.4
where the time goes:
time: 213 us
  waiting for transfers between devices  149 us (70%)
  blocking collectives  38.4 us (18%)
  between operations  14.1 us (7%)
  matrix products  8.19 us (4%)
    all_gather x1, waiting for transfers between devices, score_rows(): lax.all_gather(w_first, 'seq', axis=0, tiled=True)  114 us
    psum x1, blocking collectives, per_device(): logit = lax.psum(partial_logit, ('seq', 'head'))  38.4 us
    all_gather x1, waiting for transfers between devices, per_device(): whole = lax.all_gather(hidden_states, 'head', axis=2, tiled=True)  34.3 us
    dot_general x1, matrix products, score_rows(): jnp.dot(rows, lax.all_gather(w_first, 'seq', axis=0, tiled=True), preferr...  8.19 us
  transfers between devices with their start and end apart: 2, of which 2 were waited for; matrix products, arithmetic and copies ran while one was open for 0% of the time, Pallas kernels for 0%

commit v1 on v0

--- a/solution.py
+++ b/solution.py
@@ -16,7 +16,7 @@
     offset = lax.axis_index("seq") * tok_dev
     positions = offset + jnp.arange(tok_dev, dtype=jnp.int32)
     hits = boundary[:, :, None] == positions[None, None, :]
-    whole = lax.all_gather(hidden_states, "head", axis=2, tiled=True)
+    whole = jnp.concatenate(lax.all_gather(hidden_states, "head"), axis=2)
     token_logit = score_rows(
         whole.reshape(traces * tok_dev, whole.shape[2]), w_first, b_first, w_second
     )

time: 213 us -> 213 us (level)
  local copies, waits for them, and re-layouts: 0.85 us -> 8.24 us
  waiting for transfers between devices: 149 us -> 142 us
    all_gather x1, waiting for transfers between devices: 114 us -> 106 us  [score_rows(): lax.all_gather(w_first, 'seq', axis=0, tiled=True)]
    all_gather x0 -> x1, local copies, waits for them, and re-layouts: none -> 4.87 us  [per_device(): whole = jnp.concatenate(lax.all_gather(hidden_states, 'head'), axis=2)]
    unnamed x6 -> x11, local copies, waits for them, and re-layouts: 0.01 us -> 2.53 us
  transfers between devices with their start and end apart: 2 -> 2, of which waited for: 2 -> 2; matrix products, arithmetic and copies ran while one was open for 0% -> 4% of each run, Pallas kernels for 0% -> 0%
where the time goes in v1:
time: 213 us
  waiting for transfers between devices  142 us (67%)
  blocking collectives  38.4 us (18%)
  between operations  14.1 us (7%)
  matrix products  8.26 us (4%)
  local copies, waits for them, and re-layouts  8.24 us (4%)
    all_gather x1, waiting for transfers between devices, score_rows(): lax.all_gather(w_first, 'seq', axis=0, tiled=True)  106 us
    psum x1, blocking collectives, per_device(): logit = lax.psum(partial_logit, ('seq', 'head'))  38.4 us
    all_gather x1, waiting for transfers between devices, per_device(): whole = jnp.concatenate(lax.all_gather(hidden_states, 'head'), axis=2)  34.3 us
    dot_general x1, matrix products, score_rows(): jnp.dot(rows, lax.all_gather(w_first, 'seq', axis=0, tiled=True), preferr...  8.26 us
    all_gather x1, local copies, waits for them, and re-layouts, per_device(): whole = jnp.concatenate(lax.all_gather(hidden_states, 'head'), axis=2)  4.87 us
  transfers between devices with their start and end apart: 2, of which 2 were waited for; matrix products, arithmetic and copies ran while one was open for 4% of the time, Pallas kernels for 0%

profile of v1, /device:TPU:0, one launch (start us, length us, event | category | flops | bytes accessed | tf_op | source)
XLA Modules:
  0.0 212.8 jit_solution(2515664572823742180)
XLA Ops:
  7.2 0.0 all-gather.6.cloned.1.call-start
  7.2 0.7 all-gather.6.cloned.1.call-update
  7.9 0.0 all-gather.4.cloned.1.call-start
  7.9 0.7 all-gather.4.cloned.1.call-update
  8.7 0.8 slice_bitcast_fusion.1
  9.4 34.3 %all-gather.6.cloned.1.call-done = bf16[32,64,896]{2,1,0:T(8,128)(2,1)} async-done(((bf16[8,64,896]{2,1,0:T(8,128)(2,1)}), bf16[32,64,896]{2,1,0:T(8,128)(2,1)}) %all-gather.6.cloned.1.call-update) | async-done | bytes 3670032 | tf_op jit(solution)/shard_map/all_gather | solution.py:19
  43.8 4.9 %copy.12 = bf16[4,8,64,896]{3,0,2,1:T(4,128)(2,1)S(1)} copy(bf16[4,8,64,896]{3,2,1,0:T(8,128)(2,1)} %bitcast.12) | data formatting | bytes 7340032 | tf_op jit(solution)/shard_map/all_gather | solution.py:19
  48.6 0.0 copy-start.3
  48.7 0.0 copy-start.4
  48.7 2.5 %copy.13 = bf16[64,8,4,896]{3,1,2,0:T(8,128)(2,1)} copy(bf16[64,8,4,896]{3,2,1,0:T(4,128)(2,1)S(1)} %bitcast.11) | data formatting | bytes 7340032
  51.2 106.3 %all-gather.4.cloned.1.call-done = bf16[3584,1024]{1,0:T(8,128)(2,1)} async-done(((bf16[448,1024]{1,0:T(8,128)(2,1)}), bf16[3584,1024]{1,0:T(8,128)(2,1)}) %all-gather.4.cloned.1.call-update) | async-done | bytes 7340048 | tf_op jit(solution)/shard_map/all_gather | solution.py:9
  157.5 0.0 copy-done.3
  157.5 0.0 copy-done.4
  157.5 0.0 copy-start
  157.5 0.0 copy-start.1
  157.5 8.3 %multiply_reduce_fusion = f32[512]{0:T(512)S(1)} fusion(bf16[512,3584]{1,0:T(8,128)(2,1)} %bitcast.13, bf16[3584,1024]{1,0:T(8,128)(2,1)} %all-gather.4.cloned.1.call-done, f32[1024]{0:T(1024)S(1)} %copy-done.3, f32[1024]{0:T(1024)S(1)} %copy-done.4), kind=kOutput, calls=%fused_computation | convolution fusion | flops 3760193024 | bytes 11020288 | tf_op jit(solution)/shard_map/dot_general | solution.py:8
  165.8 0.1 broadcast_in_dim.44
  165.8 0.0 copy-done
  165.8 0.3 select_reduce_fusion
  166.1 38.4 %psum.7 = f32[8,64]{1,0:T(8,128)S(1)} all-reduce(f32[8,64]{1,0:T(8,128)S(1)} %select_reduce_fusion), channel_id=1, replica_groups=mesh['seq'=8,'head'=4] {'seq','head'}, use_global_device_ids=true, to_apply=%region_2.3 | all-reduce | flops 512 | bytes 4096 | tf_op jit(solution)/shard_map/psum | solution.py:25
  204.5 0.0 copy-done.1
  204.5 0.1 select_reduce_fusion.3
  204.6 0.0 copy-start.2
  204.6 0.6 broadcast_select_fusion
  205.2 0.2 select_reduce_fusion.1
  205.4 0.5 sub.3
  206.0 0.0 copy-done.2
  (1 shorter events, 0.0 us)
Async XLA Ops:
  7.2 36.6 %all-gather.6.cloned.1.call-start = ((), (), s32[]{:S(2)}) async-start(), calls=%async_computation.1 | async-start | bytes 4587520 | tf_op jit(solution)/shard_map/all_gather | solution.py:19
  7.9 149.6 %all-gather.4.cloned.1.call-start = ((), (), s32[]{:S(2)}) async-start(), calls=%async_computation | async-start | bytes 8257536 | tf_op jit(solution)/shard_map/all_gather | solution.py:9
  48.6 108.8 %copy-start.3 = (f32[1024]{0:T(1024)S(1)}, f32[1024]{0:T(1024)}, u32[]{:S(2)}) copy-start(f32[1024]{0:T(1024)} %param.13) | copy-start | bytes 12292
  48.7 108.8 %copy-start.4 = (f32[1024]{0:T(1024)S(1)}, f32[1024]{0:T(1024)}, u32[]{:S(2)}) copy-start(f32[1024]{0:T(1024)} %param.12) | copy-start | bytes 12292
  157.5 8.3 %copy-start = (s32[8,64]{1,0:T(8,128)S(1)}, s32[8,64]{1,0:T(8,128)}, u32[]{:S(2)}) copy-start(s32[8,64]{1,0:T(8,128)} %param.8) | copy-start | bytes 6148
  157.5 47.0 %copy-start.1 = (s32[8,64]{1,0:T(8,128)S(1)}, s32[8,64]{1,0:T(8,128)}, u32[]{:S(2)}) copy-start(s32[8,64]{1,0:T(8,128)} %param.9) | copy-start | bytes 6148
  204.6 1.3 copy-start.2
Sparse Core Ops, SparseCore 0:
  9.5 34.1 all-gather.5
  46.0 111.4 all-gather.3

commit v2 on v0

--- a/solution.py
+++ b/solution.py
@@ -22,7 +22,7 @@
     )
     token_logit = token_logit.reshape(traces, tok_dev)
     partial_logit = jnp.sum(jnp.where(hits, token_logit[:, None, :], 0.0), axis=2)
-    logit = lax.psum(partial_logit, ("seq", "head"))
+    logit = lax.psum(lax.psum(partial_logit, "head"), "seq")
     live = valid == 1
     step_reward = jnp.where(live, logit, jnp.float32(0.0))
     trace_score = jnp.min(jnp.where(live, logit, jnp.float32(1e30)), axis=1)

time: 213 us -> 200 us (0.939)
  blocking collectives: 38.4 us -> 25.4 us
    psum x1 -> x2, blocking collectives: 38.4 us -> 25.4 us  [per_device(): logit = lax.psum(lax.psum(partial_logit, 'head'), 'seq')]
where the time goes in v2:
time: 200 us
  waiting for transfers between devices  149 us (74%)
  blocking collectives  25.4 us (13%)
  between operations  14.1 us (7%)
  matrix products  8.19 us (4%)
    all_gather x1, waiting for transfers between devices, score_rows(): lax.all_gather(w_first, 'seq', axis=0, tiled=True)  114 us
    all_gather x1, waiting for transfers between devices, per_device(): whole = lax.all_gather(hidden_states, 'head', axis=2, tiled=True)  34.3 us
    psum x2, blocking collectives, per_device(): logit = lax.psum(lax.psum(partial_logit, 'head'), 'seq')  25.4 us
    dot_general x1, matrix products, score_rows(): jnp.dot(rows, lax.all_gather(w_first, 'seq', axis=0, tiled=True), preferr...  8.19 us
  transfers between devices with their start and end apart: 2, of which 2 were waited for; matrix products, arithmetic and copies ran while one was open for 0% of the time, Pallas kernels for 0%

profile of v2, /device:TPU:0, one launch (start us, length us, event | category | flops | bytes accessed | tf_op | source)
XLA Modules:
  0.0 199.7 jit_solution(10876605371150894530)
XLA Ops:
  7.2 0.0 all-gather.3.cloned.1.call-start
  7.2 0.7 all-gather.3.cloned.1.call-update
  7.9 0.0 all-gather.5.cloned.1.call-start
  7.9 0.7 all-gather.5.cloned.1.call-update
  8.7 0.8 slice_bitcast_fusion.1
  9.4 34.3 %all-gather.3.cloned.1.call-done = bf16[8,64,3584]{2,1,0:T(8,128)(2,1)} async-done(((bf16[8,64,896]{2,1,0:T(8,128)(2,1)}), bf16[8,64,3584]{2,1,0:T(8,128)(2,1)}) %all-gather.3.cloned.1.call-update) | async-done | bytes 3670032 | tf_op jit(solution)/shard_map/all_gather | solution.py:19
  43.8 113.7 %all-gather.5.cloned.1.call-done = bf16[3584,1024]{1,0:T(8,128)(2,1)} async-done(((bf16[448,1024]{1,0:T(8,128)(2,1)}), bf16[3584,1024]{1,0:T(8,128)(2,1)}) %all-gather.5.cloned.1.call-update) | async-done | bytes 7340048 | tf_op jit(solution)/shard_map/all_gather | solution.py:9
  157.5 0.0 copy-start
  157.5 0.0 copy-start.1
  157.5 8.2 %multiply_reduce_fusion = f32[512]{0:T(512)S(1)} fusion(bf16[512,3584]{1,0:T(8,128)(2,1)} %bitcast.7, bf16[3584,1024]{1,0:T(8,128)(2,1)} %all-gather.5.cloned.1.call-done, f32[1024]{0:T(1024)} %param.13, f32[1024]{0:T(1024)} %param.12), kind=kOutput, calls=%fused_computation | convolution fusion | flops 3760193024 | bytes 11020288 | tf_op jit(solution)/shard_map/dot_general | solution.py:8
  165.7 0.1 broadcast_in_dim.44
  165.7 0.0 copy-done
  165.7 0.3 select_reduce_fusion
  166.0 5.7 %psum.14 = f32[8,64]{1,0:T(8,128)S(1)} all-reduce(f32[8,64]{1,0:T(8,128)S(1)} %select_reduce_fusion), channel_id=1, replica_groups=mesh['seq'=8,'head'=4] {'head'}, use_global_device_ids=true, to_apply=%region_2.3 | all-reduce | flops 512 | bytes 4096 | tf_op jit(solution)/shard_map/psum | solution.py:25
  171.7 19.7 %psum.15 = f32[8,64]{1,0:T(8,128)S(1)} all-reduce(f32[8,64]{1,0:T(8,128)S(1)} %psum.14), channel_id=1, replica_groups=mesh['seq'=8,'head'=4] {'seq'}, use_global_device_ids=true, to_apply=%region_3.4 | all-reduce | flops 512 | bytes 4096 | tf_op jit(solution)/shard_map/psum | solution.py:25
  191.4 0.0 copy-done.1
  191.4 0.1 select_reduce_fusion.3
  191.5 0.0 copy-start.2
  191.5 0.6 broadcast_select_fusion
  192.1 0.2 select_reduce_fusion.1
  192.3 0.5 sub.3
  192.9 0.0 copy-done.2
  (1 shorter events, 0.0 us)
Async XLA Ops:
  7.2 36.6 %all-gather.3.cloned.1.call-start = ((), (), s32[]{:S(2)}) async-start(), calls=%async_computation | async-start | bytes 4587520 | tf_op jit(solution)/shard_map/all_gather | solution.py:19
  7.9 149.6 %all-gather.5.cloned.1.call-start = ((), (), s32[]{:S(2)}) async-start(), calls=%async_computation.1 | async-start | bytes 8257536 | tf_op jit(solution)/shard_map/all_gather | solution.py:9
  157.5 8.3 %copy-start = (s32[8,64]{1,0:T(8,128)S(1)}, s32[8,64]{1,0:T(8,128)}, u32[]{:S(2)}) copy-start(s32[8,64]{1,0:T(8,128)} %param.8) | copy-start | bytes 6148
  157.5 33.9 %copy-start.1 = (s32[8,64]{1,0:T(8,128)S(1)}, s32[8,64]{1,0:T(8,128)}, u32[]{:S(2)}) copy-start(s32[8,64]{1,0:T(8,128)} %param.9) | copy-start | bytes 6148
  191.5 1.3 copy-start.2
Sparse Core Ops, SparseCore 0:
  9.5 34.1 all-gather.2
  45.9 111.4 all-gather.4
